TPU v7x, 32 devices: a whole 2x2x4 slice. The times are simulated.
32 devices in a mesh: gx: 2 (over x), gy: 4 (over y, core), gz: 4 (over z).
Axes of the slice: x: 2, y: 2, z: 4, core: 2. Of those that a mesh axis runs over, the one named last changes fastest.
Arguments:
- inputs: bfloat16 [640, 8192], P(('gx', 'gz'), 'gy'), may hold values from -6 to 6
- out_grad: bfloat16 [640, 8192], P(('gx', 'gz'), 'gy'), may hold values from -6 to 6
- gate_weight: bfloat16 [8192, 16384], P('gy', ('gx', 'gz')), may hold values from -0.0625 to 0.0625
- up_weight: bfloat16 [8192, 16384], P('gy', ('gx', 'gz')), may hold values from -0.0625 to 0.0625
- down_weight: bfloat16 [16384, 8192], P(('gx', 'gz'), 'gy'), may hold values from -0.046875 to 0.046875
Outputs:
- in_grad: bfloat16 [640, 8192], P(('gx', 'gz'), 'gy')
All inputs are finite; a program needn't handle non-finite values.
Results may differ from a plain program's by a relative error of at most 0.0049.
Values may be sent and summed in bfloat16 or wider, within the bound.
A program may use at most 128 MiB of HBM per device.

v0:
```python
import functools

import jax
import jax.numpy as jnp
from jax import lax
from jax.experimental import pallas as pl
from jax.experimental.pallas import tpu as pltpu
from jax.sharding import PartitionSpec as P

F32, BF16 = jnp.float32, jnp.bfloat16
MESH = pl.DeviceIdType.MESH
SPECS = (
    P(("gx", "gz"), "gy"),
    P(("gx", "gz"), "gy"),
    P("gy", ("gx", "gz")),
    P("gy", ("gx", "gz")),
    P(("gx", "gz"), "gy"),
)
OUT_SPEC = P(("gx", "gz"), "gy")


def contract_last(left, right):
    return lax.dot_general(left, right, (((1,), (1,)), ((), ())), preferred_element_type=F32)


def grads_of(gate, upper, hidden_grad):
    logistic = jax.nn.sigmoid(gate)
    gate_grad = hidden_grad * upper * logistic * (1.0 + gate * (1.0 - logistic))
    up_grad = hidden_grad * gate * logistic
    return gate_grad.astype(BF16), up_grad.astype(BF16)


ORDER = {0: (1, 2, 3), 1: (0, 2, 3), 2: (3, 1, 0), 3: (2, 1, 0)}
CHUNKS = 5
QUARTERS = 4
PIECES = 4


def kernel(
    rows, depth, width,
    x_hbm, og_hbm, gw_hbm, uw_hbm, dw_hbm, out_ref,
    xbuf, gw, uw, dw, pbuf, drecv, mine, ysend, yrecv, gbuf, xs, xr, wb, zs, zr,
    in_sem, w_sem, ag_recv, agx_send, agz_send, d_send, d_recv, y_send, y_recv,
    gy_send, gy_recv, gd_send, gd_recv, x_send, x_recv, z_send, z_recv,
):
    gx, gy, gz = lax.axis_index("gx"), lax.axis_index("gy"), lax.axis_index("gz")
    where_y, core = gy // 2, gy % 2
    mate = gy + 1 - 2 * core
    over = gy + 2 - 4 * where_y
    across = 1 - gx
    both = 2 * rows
    quarter = width // QUARTERS
    piece = depth // PIECES

    def remote(src, dst, send, recv, **where):
        return pltpu.make_async_remote_copy(
            src_ref=src, dst_ref=dst, send_sem=send, recv_sem=recv,
            device_id=where, device_id_type=MESH,
        )

    def slot(j):
        return pl.ds(pl.multiple_of(j * rows, 16), rows)

    def columns(q):
        return pl.ds(pl.multiple_of(q * quarter, 128), quarter)

    def gather_x(k):
        return remote(
            xbuf.at[:, slot(2 * k + 1), :], xbuf.at[:, slot(2 * k + 2), :],
            agx_send.at[k], ag_recv.at[2 * k + 2], gx=across,
        )

    def gather_z(src, dst, way, n, to):
        return remote(
            xbuf.at[:, slot(src), :], xbuf.at[:, slot(dst), :],
            agz_send.at[way, n], ag_recv.at[dst], gz=to,
        )

    def mate_sums(s, t):
        return remote(
            pbuf.at[t], drecv.at[s % 2, t], d_send.at[t], d_recv.at[s % 2, t], gy=mate
        )

    def over_sums(s, h):
        part = pl.ds(h * rows, rows)
        return remote(
            ysend.at[s, :, part, :], yrecv.at[s, :, part, :],
            y_send.at[s, h], y_recv.at[s, h], gy=over,
        )

    def over_grads(s, h, q):
        block = gbuf.at[:, slot(2 * s + h), columns(q)]
        return remote(block, block, gy_send.at[s, h], gy_recv.at[s, h], gy=over)

    def mate_grads(s, q, n):
        chunk = pl.ds(pl.multiple_of(s * both, 16), both)
        block = gbuf.at[:, chunk, columns(q)]
        return remote(block, block, gd_send.at[s, n], gd_recv.at[s, n], gy=mate)

    def out_x(s, n):
        return remote(xs.at[s, n], xr.at[s, n], x_send.at[s, n], x_recv.at[s, n], gx=across)

    def out_z(k, n, to):
        return remote(zs.at[k, n], zr.at[gz, n], z_send.at[k, n], z_recv.at[gz, n], gz=to)

    def in_z(src, n):
        return remote(zs.at[0, n], zr.at[src, n], z_send.at[0, n], z_recv.at[src, n], gz=src)

    def place_of(k):
        place = ORDER[0][k - 1]
        for z in range(1, 4):
            place = jnp.where(gz == z, ORDER[z][k - 1], place)
        return place

    def quarter_of(t):
        y_of = where_y + (1 - t % 2) * (1 - 2 * where_y)
        core_of = core + (1 - t // 2) * (1 - 2 * core)
        return 2 * y_of + core_of

    def load_weights(t):
        q = quarter_of(t)
        return [
            pltpu.make_async_copy(gw_hbm.at[:, columns(q)], gw.at[:, columns(q)], w_sem.at[0, t]),
            pltpu.make_async_copy(uw_hbm.at[:, columns(q)], uw.at[:, columns(q)], w_sem.at[1, t]),
            pltpu.make_async_copy(dw_hbm.at[columns(q), :], dw.at[columns(q), :], w_sem.at[2, t]),
        ]

    load_in = [
        pltpu.make_async_copy(ref, xbuf.at[i, slot(1), :], in_sem.at[i])
        for i, ref in enumerate((x_hbm, og_hbm))
    ]
    for copy in load_in:
        copy.start()
    for t in range(QUARTERS):
        for copy in load_weights(t):
            copy.start()

    barrier = pltpu.get_barrier_semaphore()
    pl.semaphore_signal(barrier, inc=1, device_id={"gy": mate}, device_id_type=MESH)
    pl.semaphore_signal(barrier, inc=1, device_id={"gy": over}, device_id_type=MESH)
    pl.semaphore_signal(barrier, inc=1, device_id={"gx": across}, device_id_type=MESH)
    for step in range(1, 4):
        pl.semaphore_signal(
            barrier, inc=1, device_id={"gz": (gz + step) % 4}, device_id_type=MESH
        )
    pl.semaphore_wait(barrier, 6)
    for copy in load_in:
        copy.wait()

    def landing(to, src):
        return 2 * ORDER[to].index(src) + 3

    def z_sends(z, first):
        copies = []
        for way, step in ((0, 1), (1, -1)):
            if not 0 <= z + step < 4:
                continue
            n = 0
            src = z
            while 0 <= src < 4:
                from_slot = 1 if src == z else landing(z, src)
                wave = abs(src - z)
                if wave in first:
                    copies.append(gather_z(from_slot, landing(z + step, src), way, n, z + step))
                n += 1
                src -= step
        return copies

    def at_place(z):
        return pl.when(gz == z)

    gather_x(0).start()
    for z in range(4):
        @at_place(z)
        def _(z=z):
            for copy in z_sends(z, (0,)):
                copy.start()

    def arrive(k):
        slot_k = 2 * k + 1
        gather_z(1, slot_k, 0, 0, 0 * gz).wait_recv()

    def forward_step(s):
        for z in range(4):
            @at_place(z)
            def _(z=z):
                middle = z in (1, 2)
                waits = {1: (1, 2), 2: (3,), 3: ()}[s] if middle else (s,)
                for k in waits:
                    arrive(k)
                for copy in z_sends(z, (s,)):
                    copy.start()
                for k in waits:
                    gather_x(k).start()

    def has_first(s):
        return s >= 1

    def has_second(s):
        return s <= CHUNKS - 2

    def each_half(s, act):
        pl.when(has_first(s))(lambda: act(0))
        pl.when(has_second(s))(lambda: act(1))

    def project(s):
        for step in range(1, 4):
            pl.when(s == step)(functools.partial(forward_step, step))

        @pl.when(s >= 1)
        def _():
            gather_x(s - 1).wait_recv()
            for t in range(2):
                mate_sums(s - 1, t).wait_send()

        chunk = pl.ds(pl.multiple_of(s * both, 16), both)

        def one(t, carry):
            q = quarter_of(t)

            @pl.when(s == 0)
            def _():
                for copy in load_weights(t):
                    copy.wait()

            x = xbuf[0, chunk, :]
            pbuf[t, 0] = jnp.dot(x, gw[:, columns(q)], preferred_element_type=F32)
            pbuf[t, 1] = jnp.dot(x, uw[:, columns(q)], preferred_element_type=F32)
            pbuf[t, 2] = contract_last(xbuf[1, chunk, :], dw[columns(q), :])

            @pl.when(t < 2)
            def _():
                mate_sums(s, t).start()

            @pl.when(t == 2)
            def _():
                mate_sums(s, 0).wait_recv()

                def add(r, carry):
                    part = pl.ds(pl.multiple_of(r * 16, 16), 16)
                    for i in range(3):
                        total = pbuf[2, i, part, :] + drecv[s % 2, 0, i, part, :]
                        ysend[s, i, part, :] = total.astype(BF16)
                    return carry

                lax.fori_loop(0, both // 16, add, 0)
                each_half(s, lambda h: over_sums(s, h).start())

            @pl.when(t == 3)
            def _():
                mate_sums(s, 1).wait_recv()

                def add(r, carry):
                    part = pl.ds(pl.multiple_of(r * 16, 16), 16)
                    for i in range(3):
                        mine[s % 2, i, part, :] = pbuf[3, i, part, :] + drecv[s % 2, 1, i, part, :]
                    return carry

                lax.fori_loop(0, both // 16, add, 0)

            return carry

        lax.fori_loop(0, QUARTERS, one, 0)

    def differentiate(s):
        each_half(s, lambda h: over_sums(s, h).wait_recv())

        def block(r, carry):
            part = pl.ds(pl.multiple_of(r * 16, 16), 16)
            terms = [mine[s % 2, i, part, :] + yrecv[s, i, part, :].astype(F32) for i in range(3)]
            here = pl.ds(pl.multiple_of(s * both + r * 16, 16), 16)
            gbuf[0, here, columns(gy)], gbuf[1, here, columns(gy)] = grads_of(*terms)
            return carry

        lax.fori_loop(0, both // 16, block, 0)
        each_half(s, lambda h: over_grads(s, h, gy).start())
        mate_grads(s, gy, 0).start()

    def backproject(s):
        each_half(s, lambda h: over_grads(s, h, over).wait_recv())
        mate_grads(s, over, 1).start()
        mate_grads(s, mate, 0).wait_recv()
        mate_grads(s, mate + over - gy, 1).wait_recv()
        chunk = pl.ds(pl.multiple_of(s * both, 16), both)

        def one(n, carry):
            here = pl.ds(pl.multiple_of(n * piece, 128), piece)
            part = contract_last(gbuf[0, chunk, :], gw[here, :])
            part = part + contract_last(gbuf[1, chunk, :], uw[here, :])

            @pl.when(has_first(s))
            def _():
                xs[s, n] = part[:rows].astype(BF16)

            @pl.when(has_second(s))
            def _():
                wb[s, n] = part[rows:]

            @pl.when(has_first(s))
            def _():
                out_x(s, n).start()

            return carry

        lax.fori_loop(0, PIECES, one, 0)

    def pass_on(k):
        to = place_of(1)
        for j in range(2, 4):
            to = jnp.where(k == j, place_of(j), to)

        def one(n, carry):
            out_x(k + 1, n).wait_recv()
            zs[k, n] = (wb[k, n] + xr[k + 1, n].astype(F32)).astype(BF16)
            out_z(k, n, to).start()
            return carry

        lax.fori_loop(0, PIECES, one, 0)

    def stage(s, carry):
        pl.when(s == 1)(lambda: differentiate(s - 1))
        pl.when(s < CHUNKS)(lambda: project(s))
        pl.when((s >= 2) & (s <= CHUNKS))(lambda: differentiate(s - 1))
        pl.when(s >= 5)(lambda: pass_on(s - 4))
        pl.when((s >= 2) & (s <= CHUNKS + 1))(lambda: backproject(s - 2))
        return carry

    lax.fori_loop(0, CHUNKS + 3, stage, 0)

    for n in range(PIECES):
        out_x(1, n).wait_recv()
        total = wb[0, n] + xr[1, n].astype(F32)
        for step in range(1, 4):
            src = (gz + step) % 4
            in_z(src, n).wait_recv()
            total = total + zr[src, n].astype(F32)
        out_ref[:, n * piece : (n + 1) * piece] = total.astype(BF16)

    for k in range(4):
        gather_x(k).wait_send()
    for z in range(4):
        @at_place(z)
        def _(z=z):
            for copy in z_sends(z, (0, 1, 2)):
                copy.wait_send()
    for t in range(2):
        mate_sums(CHUNKS - 1, t).wait_send()

    def drain(s, carry):
        def half(h):
            over_sums(s, h).wait_send()
            over_grads(s, h, gy).wait_send()

        each_half(s, half)
        mate_grads(s, gy, 0).wait_send()
        mate_grads(s, over, 1).wait_send()

        @pl.when(has_first(s))
        def _():
            for n in range(PIECES):
                out_x(s, n).wait_send()

        @pl.when((s >= 1) & (s <= 3))
        def _():
            for n in range(PIECES):
                out_z(s, n, (gz + 1) % 4).wait_send()

        return carry

    lax.fori_loop(0, CHUNKS, drain, 0)


def fused(inputs, out_grad, gate_weight, up_weight, down_weight):
    rows, depth = inputs.shape
    width = gate_weight.shape[1]
    both, quarter, piece = 2 * rows, width // QUARTERS, depth // PIECES
    dma = pltpu.SemaphoreType.DMA
    n = CHUNKS
    scratch = [
        pltpu.VMEM((2, n * both, depth), BF16),
        pltpu.VMEM((depth, width), BF16),
        pltpu.VMEM((depth, width), BF16),
        pltpu.VMEM((width, depth), BF16),
        pltpu.VMEM((4, 3, both, quarter), F32),
        pltpu.VMEM((2, 2, 3, both, quarter), F32),
        pltpu.VMEM((2, 3, both, quarter), F32),
        pltpu.VMEM((n, 3, both, quarter), BF16),
        pltpu.VMEM((n, 3, both, quarter), BF16),
        pltpu.VMEM((2, n * both, width), BF16),
        pltpu.VMEM((n, PIECES, rows, piece), BF16),
        pltpu.VMEM((n, PIECES, rows, piece), BF16),
        pltpu.VMEM((4, PIECES, rows, piece), F32),
        pltpu.VMEM((4, PIECES, rows, piece), BF16),
        pltpu.VMEM((4, PIECES, rows, piece), BF16),
        dma((2,)), dma((3, 4)), dma((2 * n,)), dma((4,)), dma((2, 4)), dma((2,)), dma((2, 2)),
        dma((n, 2)), dma((n, 2)), dma((n, 2)), dma((n, 2)), dma((n, 2)), dma((n, 2)),
        dma((n, PIECES)), dma((n, PIECES)), dma((4, PIECES)), dma((4, PIECES)),
    ]
    return pl.pallas_call(
        functools.partial(kernel, rows, depth, width),
        out_shape=jax.ShapeDtypeStruct((rows, depth), BF16),
        in_specs=[pl.BlockSpec(memory_space=pl.ANY)] * 5,
        out_specs=pl.BlockSpec(memory_space=pltpu.VMEM),
        scratch_shapes=scratch,
        compiler_params=pltpu.CompilerParams(
            collective_id=0, has_side_effects=True, vmem_limit_bytes=66 * 1024 * 1000
        ),
    )(inputs, out_grad, gate_weight, up_weight, down_weight)


def plain(nx, ny, nz):
    def layer(inputs, out_grad, gate_weight, up_weight, down_weight):
        both = lax.all_gather(jnp.stack([inputs, out_grad]), ("gx", "gz"), axis=1, tiled=True)
        gate = jnp.dot(both[0], gate_weight, preferred_element_type=F32)
        upper = jnp.dot(both[0], up_weight, preferred_element_type=F32)
        hidden = contract_last(both[1], down_weight)
        terms = lax.psum_scatter(
            jnp.stack([gate, upper, hidden]), "gy", scatter_dimension=1, tiled=True
        )
        grads = jnp.stack(grads_of(terms[0], terms[1], terms[2]))
        grads = lax.all_gather(grads, "gy", axis=1, tiled=True)
        total = contract_last(grads[0], gate_weight) + contract_last(grads[1], up_weight)
        total = lax.psum_scatter(total, ("gx", "gz"), scatter_dimension=0, tiled=True)
        return total.astype(BF16)

    return layer


def solution(mesh):
    nx, ny, nz = mesh.shape["gx"], mesh.shape["gy"], mesh.shape["gz"]
    body = fused if (nx, ny, nz) == (2, 4, 4) else plain(nx, ny, nz)
    return jax.shard_map(body, mesh=mesh, in_specs=SPECS, out_specs=OUT_SPEC, check_vma=False)
```

profile of v0, /device:TPU:0, one launch (start us, length us, event | category | flops | bytes accessed | tf_op | source)
XLA Modules:
  0.0 139.8 jit_solution(13646310000636617851)
XLA Ops:
  0.0 138.0 %shard_map.55 = bf16[80,2048]{1,0:T(8,128)(2,1)} custom-call(bf16[80,2048]{1,0:T(8,128)(2,1)} %x_hbm.1, bf16[80,2048]{1,0:T(8,128)(2,1)} %og_hbm.1, bf16[2048,2048]{1,0:T(8,128)(2,1)} %gw_hbm.1, bf16[2048,2048]{1,0:T(8,128)(2,1)} %uw_hbm.1, bf16[2048,2048]{1,0:T(8,128)(2,1)} %dw_hbm.1), custom_call_target="tpu_custom_call" | custom-call | tf_op jit(solution)/shard_map/pallas_call | solution.py:399
  138.0 1.7 %copy.7 = bf16[80,2048]{1,0:T(8,128)(2,1)} copy(bf16[80,2048]{1,0:T(8,128)(2,1)} %shard_map.55) | data formatting | bytes 655360
where the time goes:
time: 140 us
  Pallas kernels  138 us (99%)
  local copies, waits for them, and re-layouts  1.72 us (1%)
    pallas_call x1, Pallas kernels, fused(): pl.pallas_call(functools.partial(kernel, rows, depth, width), out_shape=j...  138 us

commit v1 on v0

--- a/solution.py
+++ b/solution.py
@@ -39,15 +39,17 @@
 def kernel(
     rows, depth, width,
     x_hbm, og_hbm, gw_hbm, uw_hbm, dw_hbm, out_ref,
-    xbuf, gw, uw, dw, pbuf, drecv, mine, ysend, yrecv, gbuf, xs, xr, wb, zs, zr,
+    xbuf, gw, uw, dw, pbuf, drecv, mine, ysend, yrecv, gbuf, xs, xr, wb, zs, zr, zm,
     in_sem, w_sem, ag_recv, agx_send, agz_send, d_send, d_recv, y_send, y_recv,
-    gy_send, gy_recv, gd_send, gd_recv, x_send, x_recv, z_send, z_recv,
+    gy_send, gy_recv, gd_send, gd_recv, x_send, x_recv, z_send, z_recv, zm_recv,
 ):
     gx, gy, gz = lax.axis_index("gx"), lax.axis_index("gy"), lax.axis_index("gz")
     where_y, core = gy // 2, gy % 2
     mate = gy + 1 - 2 * core
     over = gy + 2 - 4 * where_y
     across = 1 - gx
+    near = gz + 1 - 2 * (gz % 2)
+    middle = (gz == 1) | (gz == 2)
     both = 2 * rows
     quarter = width // QUARTERS
     piece = depth // PIECES
@@ -88,29 +90,24 @@
             y_send.at[s, h], y_recv.at[s, h], gy=over,
         )
 
-    def over_grads(s, h, q):
-        block = gbuf.at[:, slot(2 * s + h), columns(q)]
-        return remote(block, block, gy_send.at[s, h], gy_recv.at[s, h], gy=over)
-
-    def mate_grads(s, q, n):
-        chunk = pl.ds(pl.multiple_of(s * both, 16), both)
-        block = gbuf.at[:, chunk, columns(q)]
-        return remote(block, block, gd_send.at[s, n], gd_recv.at[s, n], gy=mate)
-
-    def out_x(s, n):
-        return remote(xs.at[s, n], xr.at[s, n], x_send.at[s, n], x_recv.at[s, n], gx=across)
-
-    def out_z(k, n, to):
-        return remote(zs.at[k, n], zr.at[gz, n], z_send.at[k, n], z_recv.at[gz, n], gz=to)
-
-    def in_z(src, n):
-        return remote(zs.at[0, n], zr.at[src, n], z_send.at[0, n], z_recv.at[src, n], gz=src)
-
-    def place_of(k):
-        place = ORDER[0][k - 1]
-        for z in range(1, 4):
-            place = jnp.where(gz == z, ORDER[z][k - 1], place)
-        return place
+    def over_grads(j, q):
+        block = gbuf.at[:, slot(j), columns(q)]
+        return remote(block, block, gy_send.at[j], gy_recv.at[j], gy=over)
+
+    def mate_grads(j, q, n):
+        block = gbuf.at[:, slot(j), columns(q)]
+        return remote(block, block, gd_send.at[j, n], gd_recv.at[j, n], gy=mate)
+
+    def out_x(k, n):
+        return remote(xs.at[k, n], xr.at[k, n], x_send.at[k, n], x_recv.at[k, n], gx=across)
+
+    def to_owner(k, n, lane, to):
+        return remote(zs.at[k, n], zr.at[lane, n], z_send.at[k, n], z_recv.at[lane, n], gz=to)
+
+    def to_middle(k, n):
+        return remote(
+            zs.at[k, n], zm.at[k - 2, n], z_send.at[k, n], zm_recv.at[k - 2, n], gz=near
+        )
 
     def quarter_of(t):
         y_of = where_y + (1 - t % 2) * (1 - 2 * where_y)
@@ -131,9 +128,6 @@
     ]
     for copy in load_in:
         copy.start()
-    for t in range(QUARTERS):
-        for copy in load_weights(t):
-            copy.start()
 
     barrier = pltpu.get_barrier_semaphore()
     pl.semaphore_signal(barrier, inc=1, device_id={"gy": mate}, device_id_type=MESH)
@@ -143,9 +137,12 @@
         pl.semaphore_signal(
             barrier, inc=1, device_id={"gz": (gz + step) % 4}, device_id_type=MESH
         )
-    pl.semaphore_wait(barrier, 6)
     for copy in load_in:
         copy.wait()
+    for t in range(QUARTERS):
+        for copy in load_weights(t):
+            copy.start()
+    pl.semaphore_wait(barrier, 6)
 
     def landing(to, src):
         return 2 * ORDER[to].index(src) + 3
@@ -204,9 +201,6 @@
         pl.when(has_second(s))(lambda: act(1))
 
     def project(s):
-        for step in range(1, 4):
-            pl.when(s == step)(functools.partial(forward_step, step))
-
         @pl.when(s >= 1)
         def _():
             gather_x(s - 1).wait_recv()
@@ -273,67 +267,111 @@
             return carry
 
         lax.fori_loop(0, both // 16, block, 0)
-        each_half(s, lambda h: over_grads(s, h, gy).start())
-        mate_grads(s, gy, 0).start()
-
-    def backproject(s):
-        each_half(s, lambda h: over_grads(s, h, over).wait_recv())
-        mate_grads(s, over, 1).start()
-        mate_grads(s, mate, 0).wait_recv()
-        mate_grads(s, mate + over - gy, 1).wait_recv()
-        chunk = pl.ds(pl.multiple_of(s * both, 16), both)
+        each_half(s, lambda h: mate_grads(2 * s + h, gy, 0).start())
+
+    def hand_over(*slots):
+        for j in slots:
+            over_grads(j, gy).start()
+
+    def backproject(k, s):
+        for h in (1, 2):
+            over_grads(2 * k + h, over).wait_recv()
+            mate_grads(2 * k + h, over, 1).start()
+        for h in (1, 2):
+            mate_grads(2 * k + h, mate, 0).wait_recv()
+            mate_grads(2 * k + h, mate + over - gy, 1).wait_recv()
+        pair = pl.ds(pl.multiple_of((2 * k + 1) * rows, 16), both)
 
         def one(n, carry):
             here = pl.ds(pl.multiple_of(n * piece, 128), piece)
-            part = contract_last(gbuf[0, chunk, :], gw[here, :])
-            part = part + contract_last(gbuf[1, chunk, :], uw[here, :])
-
-            @pl.when(has_first(s))
-            def _():
-                xs[s, n] = part[:rows].astype(BF16)
-
-            @pl.when(has_second(s))
-            def _():
-                wb[s, n] = part[rows:]
-
-            @pl.when(has_first(s))
-            def _():
-                out_x(s, n).start()
+            part = contract_last(gbuf[0, pair, :], gw[here, :])
+            part = part + contract_last(gbuf[1, pair, :], uw[here, :])
+            xs[k, n] = part[rows:].astype(BF16)
+            wb[k, n] = part[:rows]
+            out_x(k, n).start()
+
+            @pl.when((s == 5) & jnp.logical_not(middle))
+            def _():
+                pass_to_middle(2, n)
+
+            @pl.when(s == 6)
+            def _():
+                pl.when(middle)(lambda: pass_from_middle(2, n))
+                pass_near(n)
 
             return carry
 
         lax.fori_loop(0, PIECES, one, 0)
 
-    def pass_on(k):
-        to = place_of(1)
-        for j in range(2, 4):
-            to = jnp.where(k == j, place_of(j), to)
-
-        def one(n, carry):
-            out_x(k + 1, n).wait_recv()
-            zs[k, n] = (wb[k, n] + xr[k + 1, n].astype(F32)).astype(BF16)
-            out_z(k, n, to).start()
-            return carry
-
-        lax.fori_loop(0, PIECES, one, 0)
+    def paired(k, n):
+        out_x(k, n).wait_recv()
+        return wb[k, n] + xr[k, n].astype(F32)
+
+    def pass_near(n):
+        zs[1, n] = paired(1, n).astype(BF16)
+        to_owner(1, n, 0, near).start()
+
+    def pass_to_middle(k, n):
+        zs[k, n] = paired(k, n).astype(BF16)
+        to_middle(k, n).start()
+
+    def pass_from_middle(k, n):
+        total = paired(k, n)
+        to_middle(k, n).wait_recv()
+        zs[k, n] = (total + zm[k - 2, n].astype(F32)).astype(BF16)
+        to_owner(k, n, 1, 3 - gz if k == 2 else (gz + 2) % 4).start()
 
     def stage(s, carry):
-        pl.when(s == 1)(lambda: differentiate(s - 1))
+        pl.when(s == 2)(lambda: forward_step(2))
+        pl.when(s == 3)(lambda: forward_step(3))
+
+        @pl.when((s == 1) | (s == 2) | (s == 4))
+        def _():
+            differentiate(s - 1)
+
+        @pl.when(s == 1)
+        def _():
+            hand_over(1)
+            forward_step(1)
+
+        pl.when(s == 2)(lambda: hand_over(2))
+        pl.when(s == 4)(lambda: hand_over(6))
         pl.when(s < CHUNKS)(lambda: project(s))
-        pl.when((s >= 2) & (s <= CHUNKS))(lambda: differentiate(s - 1))
-        pl.when(s >= 5)(lambda: pass_on(s - 4))
-        pl.when((s >= 2) & (s <= CHUNKS + 1))(lambda: backproject(s - 2))
+        pl.when(s == 2)(lambda: hand_over(3))
+
+        @pl.when(s == 3)
+        def _():
+            differentiate(2)
+            hand_over(5)
+
+        pl.when(s == 4)(lambda: hand_over(4, 7))
+
+        @pl.when(s >= 3)
+        def _():
+            backproject(s - 3 + (s == 4).astype(jnp.int32) - (s == 5).astype(jnp.int32), s)
+
+        @pl.when(s == 4)
+        def _():
+            differentiate(4)
+            hand_over(8)
+
         return carry
 
-    lax.fori_loop(0, CHUNKS + 3, stage, 0)
+    lax.fori_loop(0, CHUNKS + 2, stage, 0)
+
+    def last(n, carry):
+        pl.when(middle)(lambda: pass_from_middle(3, n))
+        pl.when(jnp.logical_not(middle))(lambda: pass_to_middle(3, n))
+        return carry
+
+    lax.fori_loop(0, PIECES, last, 0)
 
     for n in range(PIECES):
-        out_x(1, n).wait_recv()
-        total = wb[0, n] + xr[1, n].astype(F32)
-        for step in range(1, 4):
-            src = (gz + step) % 4
-            in_z(src, n).wait_recv()
-            total = total + zr[src, n].astype(F32)
+        out_x(0, n).wait_recv()
+        total = wb[0, n] + xr[0, n].astype(F32)
+        for lane in range(2):
+            to_owner(1, n, lane, near).wait_recv()
+            total = total + zr[lane, n].astype(F32)
         out_ref[:, n * piece : (n + 1) * piece] = total.astype(BF16)
 
     for k in range(4):
@@ -346,28 +384,30 @@
     for t in range(2):
         mate_sums(CHUNKS - 1, t).wait_send()
 
-    def drain(s, carry):
-        def half(h):
-            over_sums(s, h).wait_send()
-            over_grads(s, h, gy).wait_send()
-
-        each_half(s, half)
-        mate_grads(s, gy, 0).wait_send()
-        mate_grads(s, over, 1).wait_send()
-
-        @pl.when(has_first(s))
+    def drain_sums(s, carry):
+        each_half(s, lambda h: over_sums(s, h).wait_send())
+        return carry
+
+    def drain_grads(j, carry):
+        over_grads(j, gy).wait_send()
+        for n in range(2):
+            mate_grads(j, gy, n).wait_send()
+        return carry
+
+    def drain_out(k, carry):
+        for n in range(PIECES):
+            out_x(k, n).wait_send()
+
+        @pl.when(k >= 1)
         def _():
             for n in range(PIECES):
-                out_x(s, n).wait_send()
-
-        @pl.when((s >= 1) & (s <= 3))
-        def _():
-            for n in range(PIECES):
-                out_z(s, n, (gz + 1) % 4).wait_send()
+                to_owner(k, n, 0, near).wait_send()
 
         return carry
 
-    lax.fori_loop(0, CHUNKS, drain, 0)
+    lax.fori_loop(0, CHUNKS, drain_sums, 0)
+    lax.fori_loop(1, 2 * CHUNKS - 1, drain_grads, 0)
+    lax.fori_loop(0, 4, drain_out, 0)
 
 
 def fused(inputs, out_grad, gate_weight, up_weight, down_weight):
@@ -387,14 +427,15 @@
         pltpu.VMEM((n, 3, both, quarter), BF16),
         pltpu.VMEM((n, 3, both, quarter), BF16),
         pltpu.VMEM((2, n * both, width), BF16),
-        pltpu.VMEM((n, PIECES, rows, piece), BF16),
-        pltpu.VMEM((n, PIECES, rows, piece), BF16),
+        pltpu.VMEM((4, PIECES, rows, piece), BF16),
+        pltpu.VMEM((4, PIECES, rows, piece), BF16),
         pltpu.VMEM((4, PIECES, rows, piece), F32),
         pltpu.VMEM((4, PIECES, rows, piece), BF16),
-        pltpu.VMEM((4, PIECES, rows, piece), BF16),
+        pltpu.VMEM((2, PIECES, rows, piece), BF16),
+        pltpu.VMEM((2, PIECES, rows, piece), BF16),
         dma((2,)), dma((3, 4)), dma((2 * n,)), dma((4,)), dma((2, 4)), dma((2,)), dma((2, 2)),
-        dma((n, 2)), dma((n, 2)), dma((n, 2)), dma((n, 2)), dma((n, 2)), dma((n, 2)),
-        dma((n, PIECES)), dma((n, PIECES)), dma((4, PIECES)), dma((4, PIECES)),
+        dma((n, 2)), dma((n, 2)), dma((2 * n,)), dma((2 * n,)), dma((2 * n, 2)), dma((2 * n, 2)),
+        dma((4, PIECES)), dma((4, PIECES)), dma((4, PIECES)), dma((2, PIECES)), dma((2, PIECES)),
     ]
     return pl.pallas_call(
         functools.partial(kernel, rows, depth, width),

time: 140 us -> 121 us (0.86)
  Pallas kernels: 138 us -> 119 us
    pallas_call x1, Pallas kernels: 138 us -> 119 us  [fused(): pl.pallas_call(functools.partial(kernel, rows, depth, width), out_shape=j...]
where the time goes in v1:
time: 121 us
  Pallas kernels  119 us (98%)
  local copies, waits for them, and re-layouts  1.72 us (1%)
    pallas_call x1, Pallas kernels, fused(): pl.pallas_call(functools.partial(kernel, rows, depth, width), out_shape=j...  119 us

profile of v1, /device:TPU:0, one launch (start us, length us, event | category | flops | bytes accessed | tf_op | source)
XLA Modules:
  0.0 121.0 jit_solution(18033968190087611035)
XLA Ops:
  0.0 119.3 %shard_map.55 = bf16[80,2048]{1,0:T(8,128)(2,1)} custom-call(bf16[80,2048]{1,0:T(8,128)(2,1)} %x_hbm.1, bf16[80,2048]{1,0:T(8,128)(2,1)} %og_hbm.1, bf16[2048,2048]{1,0:T(8,128)(2,1)} %gw_hbm.1, bf16[2048,2048]{1,0:T(8,128)(2,1)} %uw_hbm.1, bf16[2048,2048]{1,0:T(8,128)(2,1)} %dw_hbm.1), custom_call_target="tpu_custom_call" | custom-call | tf_op jit(solution)/shard_map/pallas_call | solution.py:440
  119.3 1.7 %copy.7 = bf16[80,2048]{1,0:T(8,128)(2,1)} copy(bf16[80,2048]{1,0:T(8,128)(2,1)} %shard_map.55) | data formatting | bytes 655360

commit v2 on v1

--- a/solution.py
+++ b/solution.py
@@ -34,6 +34,7 @@
 CHUNKS = 5
 QUARTERS = 4
 PIECES = 4
+SENDS = 8
 
 
 def kernel(
@@ -41,7 +42,7 @@
     x_hbm, og_hbm, gw_hbm, uw_hbm, dw_hbm, out_ref,
     xbuf, gw, uw, dw, pbuf, drecv, mine, ysend, yrecv, gbuf, xs, xr, wb, zs, zr, zm,
     in_sem, w_sem, ag_recv, agx_send, agz_send, d_send, d_recv, y_send, y_recv,
-    gy_send, gy_recv, gd_send, gd_recv, x_send, x_recv, z_send, z_recv, zm_recv,
+    gy_send, gy_recv, gd_send, gd_recv, x_send, x_recv, z_send, z_recv, zm_recv, obuf, o_sem,
 ):
     gx, gy, gz = lax.axis_index("gx"), lax.axis_index("gy"), lax.axis_index("gz")
     where_y, core = gy // 2, gy % 2
@@ -52,7 +53,8 @@
     middle = (gz == 1) | (gz == 2)
     both = 2 * rows
     quarter = width // QUARTERS
-    piece = depth // PIECES
+    piece, strip = depth // PIECES, depth // SENDS
+    per = SENDS // PIECES
 
     def remote(src, dst, send, recv, **where):
         return pltpu.make_async_remote_copy(
@@ -286,22 +288,31 @@
             here = pl.ds(pl.multiple_of(n * piece, 128), piece)
             part = contract_last(gbuf[0, pair, :], gw[here, :])
             part = part + contract_last(gbuf[1, pair, :], uw[here, :])
-            xs[k, n] = part[rows:].astype(BF16)
-            wb[k, n] = part[:rows]
-            out_x(k, n).start()
-
-            @pl.when((s == 5) & jnp.logical_not(middle))
-            def _():
-                pass_to_middle(2, n)
-
-            @pl.when(s == 6)
-            def _():
-                pl.when(middle)(lambda: pass_from_middle(2, n))
-                pass_near(n)
-
+            for i in range(per):
+                m = n * per + i
+                xs[k, m] = part[rows:, i * strip : (i + 1) * strip].astype(BF16)
+                wb[k, m] = part[:rows, i * strip : (i + 1) * strip]
+                out_x(k, m).start()
+
+            pl.when((s == 5) & middle)(lambda: from_middle(2, n))
+            pl.when((s == 5) & (n < 2) & jnp.logical_not(middle))(lambda: into_middle(2, n + 2))
+            pl.when((s == 6) & (n < 2))(lambda: to_near(n + 2))
+            pl.when((s == 6) & (n >= 2) & jnp.logical_not(middle))(lambda: into_middle(3, n - 2))
             return carry
 
         lax.fori_loop(0, PIECES, one, 0)
+
+    def to_near(n):
+        for i in range(per):
+            pass_near(n * per + i)
+
+    def into_middle(k, n):
+        for i in range(per):
+            pass_to_middle(k, n * per + i)
+
+    def from_middle(k, n):
+        for i in range(per):
+            pass_from_middle(k, n * per + i)
 
     def paired(k, n):
         out_x(k, n).wait_recv()
@@ -348,31 +359,54 @@
 
         @pl.when(s >= 3)
         def _():
-            backproject(s - 3 + (s == 4).astype(jnp.int32) - (s == 5).astype(jnp.int32), s)
+            pair = jnp.where(s == 4, 2, jnp.where(s == 5, 1, s - 3))
+            backproject(pair, s)
 
         @pl.when(s == 4)
         def _():
             differentiate(4)
             hand_over(8)
 
+            @pl.when(jnp.logical_not(middle))
+            def _():
+                for n in range(2):
+                    into_middle(2, n)
+
+        @pl.when(s == 5)
+        def _():
+            for n in range(2):
+                to_near(n)
+
         return carry
 
     lax.fori_loop(0, CHUNKS + 2, stage, 0)
 
-    def last(n, carry):
-        pl.when(middle)(lambda: pass_from_middle(3, n))
-        pl.when(jnp.logical_not(middle))(lambda: pass_to_middle(3, n))
-        return carry
-
-    lax.fori_loop(0, PIECES, last, 0)
-
-    for n in range(PIECES):
+    @pl.when(middle)
+    def _():
+        for n in range(PIECES):
+            from_middle(3, n)
+
+    @pl.when(jnp.logical_not(middle))
+    def _():
+        for n in (PIECES - 2, PIECES - 1):
+            into_middle(3, n)
+
+    def out_copy(n):
+        return pltpu.make_async_copy(
+            obuf.at[n], out_ref.at[:, pl.ds(pl.multiple_of(n * strip, 128), strip)], o_sem.at[n]
+        )
+
+    def finish(n, carry):
         out_x(0, n).wait_recv()
         total = wb[0, n] + xr[0, n].astype(F32)
         for lane in range(2):
             to_owner(1, n, lane, near).wait_recv()
             total = total + zr[lane, n].astype(F32)
-        out_ref[:, n * piece : (n + 1) * piece] = total.astype(BF16)
+        obuf[n] = total.astype(BF16)
+        out_copy(n).start()
+        return carry
+
+    lax.fori_loop(0, SENDS, finish, 0)
 
     for k in range(4):
         gather_x(k).wait_send()
@@ -395,12 +429,12 @@
         return carry
 
     def drain_out(k, carry):
-        for n in range(PIECES):
+        for n in range(SENDS):
             out_x(k, n).wait_send()
 
         @pl.when(k >= 1)
         def _():
-            for n in range(PIECES):
+            for n in range(SENDS):
                 to_owner(k, n, 0, near).wait_send()
 
         return carry
@@ -408,12 +442,14 @@
     lax.fori_loop(0, CHUNKS, drain_sums, 0)
     lax.fori_loop(1, 2 * CHUNKS - 1, drain_grads, 0)
     lax.fori_loop(0, 4, drain_out, 0)
+    for n in range(SENDS):
+        out_copy(n).wait()
 
 
 def fused(inputs, out_grad, gate_weight, up_weight, down_weight):
     rows, depth = inputs.shape
     width = gate_weight.shape[1]
-    both, quarter, piece = 2 * rows, width // QUARTERS, depth // PIECES
+    both, quarter, strip = 2 * rows, width // QUARTERS, depth // SENDS
     dma = pltpu.SemaphoreType.DMA
     n = CHUNKS
     scratch = [
@@ -427,21 +463,22 @@
         pltpu.VMEM((n, 3, both, quarter), BF16),
         pltpu.VMEM((n, 3, both, quarter), BF16),
         pltpu.VMEM((2, n * both, width), BF16),
-        pltpu.VMEM((4, PIECES, rows, piece), BF16),
-        pltpu.VMEM((4, PIECES, rows, piece), BF16),
-        pltpu.VMEM((4, PIECES, rows, piece), F32),
-        pltpu.VMEM((4, PIECES, rows, piece), BF16),
-        pltpu.VMEM((2, PIECES, rows, piece), BF16),
-        pltpu.VMEM((2, PIECES, rows, piece), BF16),
+        pltpu.VMEM((4, SENDS, rows, strip), BF16),
+        pltpu.VMEM((4, SENDS, rows, strip), BF16),
+        pltpu.VMEM((4, SENDS, rows, strip), F32),
+        pltpu.VMEM((4, SENDS, rows, strip), BF16),
+        pltpu.VMEM((2, SENDS, rows, strip), BF16),
+        pltpu.VMEM((2, SENDS, rows, strip), BF16),
         dma((2,)), dma((3, 4)), dma((2 * n,)), dma((4,)), dma((2, 4)), dma((2,)), dma((2, 2)),
         dma((n, 2)), dma((n, 2)), dma((2 * n,)), dma((2 * n,)), dma((2 * n, 2)), dma((2 * n, 2)),
-        dma((4, PIECES)), dma((4, PIECES)), dma((4, PIECES)), dma((2, PIECES)), dma((2, PIECES)),
+        dma((4, SENDS)), dma((4, SENDS)), dma((4, SENDS)), dma((2, SENDS)), dma((2, SENDS)),
+        pltpu.VMEM((SENDS, rows, strip), BF16), dma((SENDS,)),
     ]
     return pl.pallas_call(
         functools.partial(kernel, rows, depth, width),
         out_shape=jax.ShapeDtypeStruct((rows, depth), BF16),
         in_specs=[pl.BlockSpec(memory_space=pl.ANY)] * 5,
-        out_specs=pl.BlockSpec(memory_space=pltpu.VMEM),
+        out_specs=pl.BlockSpec(memory_space=pl.ANY),
         scratch_shapes=scratch,
         compiler_params=pltpu.CompilerParams(
             collective_id=0, has_side_effects=True, vmem_limit_bytes=66 * 1024 * 1000

time: 121 us -> 118 us (0.975)
  Pallas kernels: 119 us -> 116 us
    pallas_call x1, Pallas kernels: 119 us -> 116 us  [fused(): pl.pallas_call(functools.partial(kernel, rows, depth, width), out_shape=j...]
where the time goes in v2:
time: 118 us
  Pallas kernels  116 us (98%)
  local copies, waits for them, and re-layouts  1.72 us (1%)
    pallas_call x1, Pallas kernels, fused(): pl.pallas_call(functools.partial(kernel, rows, depth, width), out_shape=j...  116 us

profile of v2, /device:TPU:0, one launch (start us, length us, event | category | flops | bytes accessed | tf_op | source)
XLA Modules:
  0.0 117.5 jit_solution(1618798520995508451)
XLA Ops:
  0.0 115.8 %shard_map.55 = bf16[80,2048]{1,0:T(8,128)(2,1)} custom-call(bf16[80,2048]{1,0:T(8,128)(2,1)} %x_hbm.1, bf16[80,2048]{1,0:T(8,128)(2,1)} %og_hbm.1, bf16[2048,2048]{1,0:T(8,128)(2,1)} %gw_hbm.1, bf16[2048,2048]{1,0:T(8,128)(2,1)} %uw_hbm.1, bf16[2048,2048]{1,0:T(8,128)(2,1)} %dw_hbm.1), custom_call_target="tpu_custom_call" | custom-call | tf_op jit(solution)/shard_map/pallas_call | solution.py:477
  115.8 1.7 %copy.7 = bf16[80,2048]{1,0:T(8,128)(2,1)} copy(bf16[80,2048]{1,0:T(8,128)(2,1)} %shard_map.55) | data formatting | bytes 655360

commit v3 on v2

--- a/solution.py
+++ b/solution.py
@@ -286,8 +286,9 @@
 
         def one(n, carry):
             here = pl.ds(pl.multiple_of(n * piece, 128), piece)
-            part = contract_last(gbuf[0, pair, :], gw[here, :])
-            part = part + contract_last(gbuf[1, pair, :], uw[here, :])
+            grads = jnp.concatenate([gbuf[0, pair, :], gbuf[1, pair, :]], axis=1)
+            weights = jnp.concatenate([gw[here, :], uw[here, :]], axis=1)
+            part = contract_last(grads, weights)
             for i in range(per):
                 m = n * per + i
                 xs[k, m] = part[rows:, i * strip : (i + 1) * strip].astype(BF16)
@@ -395,6 +396,41 @@
         return pltpu.make_async_copy(
             obuf.at[n], out_ref.at[:, pl.ds(pl.multiple_of(n * strip, 128), strip)], o_sem.at[n]
         )
+
+    for k in range(4):
+        gather_x(k).wait_send()
+    for z in range(4):
+        @at_place(z)
+        def _(z=z):
+            for copy in z_sends(z, (0, 1, 2)):
+                copy.wait_send()
+    for t in range(2):
+        mate_sums(CHUNKS - 1, t).wait_send()
+
+    def drain_sums(s, carry):
+        each_half(s, lambda h: over_sums(s, h).wait_send())
+        return carry
+
+    def drain_grads(j, carry):
+        over_grads(j, gy).wait_send()
+        for n in range(2):
+            mate_grads(j, gy, n).wait_send()
+        return carry
+
+    def drain_out(k, carry):
+        for n in range(SENDS):
+            out_x(k, n).wait_send()
+
+        @pl.when((k == 1) | (k == 2))
+        def _():
+            for n in range(SENDS):
+                to_owner(k, n, 0, near).wait_send()
+
+        return carry
+
+    lax.fori_loop(0, CHUNKS, drain_sums, 0)
+    lax.fori_loop(1, 2 * CHUNKS - 1, drain_grads, 0)
+    lax.fori_loop(0, 4, drain_out, 0)
 
     def finish(n, carry):
         out_x(0, n).wait_recv()
@@ -408,40 +444,8 @@
 
     lax.fori_loop(0, SENDS, finish, 0)
 
-    for k in range(4):
-        gather_x(k).wait_send()
-    for z in range(4):
-        @at_place(z)
-        def _(z=z):
-            for copy in z_sends(z, (0, 1, 2)):
-                copy.wait_send()
-    for t in range(2):
-        mate_sums(CHUNKS - 1, t).wait_send()
-
-    def drain_sums(s, carry):
-        each_half(s, lambda h: over_sums(s, h).wait_send())
-        return carry
-
-    def drain_grads(j, carry):
-        over_grads(j, gy).wait_send()
-        for n in range(2):
-            mate_grads(j, gy, n).wait_send()
-        return carry
-
-    def drain_out(k, carry):
-        for n in range(SENDS):
-            out_x(k, n).wait_send()
-
-        @pl.when(k >= 1)
-        def _():
-            for n in range(SENDS):
-                to_owner(k, n, 0, near).wait_send()
-
-        return carry
-
-    lax.fori_loop(0, CHUNKS, drain_sums, 0)
-    lax.fori_loop(1, 2 * CHUNKS - 1, drain_grads, 0)
-    lax.fori_loop(0, 4, drain_out, 0)
+    for n in range(SENDS):
+        to_owner(3, n, 0, near).wait_send()
     for n in range(SENDS):
         out_copy(n).wait()
 

time: 118 us -> 118 us (level)
  no operation moved by 1% of the time
where the time goes in v3:
time: 118 us
  Pallas kernels  116 us (98%)
  local copies, waits for them, and re-layouts  1.72 us (1%)
    pallas_call x1, Pallas kernels, fused(): pl.pallas_call(functools.partial(kernel, rows, depth, width), out_shape=j...  116 us

profile of v3, /device:TPU:0, one launch (start us, length us, event | category | flops | bytes accessed | tf_op | source)
XLA Modules:
  0.0 117.5 jit_solution(5808798972527648116)
XLA Ops:
  0.0 115.8 %shard_map.55 = bf16[80,2048]{1,0:T(8,128)(2,1)} custom-call(bf16[80,2048]{1,0:T(8,128)(2,1)} %x_hbm.1, bf16[80,2048]{1,0:T(8,128)(2,1)} %og_hbm.1, bf16[2048,2048]{1,0:T(8,128)(2,1)} %gw_hbm.1, bf16[2048,2048]{1,0:T(8,128)(2,1)} %uw_hbm.1, bf16[2048,2048]{1,0:T(8,128)(2,1)} %dw_hbm.1), custom_call_target="tpu_custom_call" | custom-call | tf_op jit(solution)/shard_map/pallas_call | solution.py:481
  115.8 1.7 %copy.7 = bf16[80,2048]{1,0:T(8,128)(2,1)} copy(bf16[80,2048]{1,0:T(8,128)(2,1)} %shard_map.55) | data formatting | bytes 655360
